TPU v7x, 32 devices: a whole 2x2x4 slice. The times are simulated.
32 devices in a mesh: member: 4 (over x, core), region: 8 (over z, y).
Axes of the slice: x: 2, y: 2, z: 4, core: 2. Of those that a mesh axis runs over, the one named last changes fastest.
Arguments:
- ensemble: float32 [12, 16, 32, 512], P('member', 'region'), may hold values from -6 to 6
- obs_value: float32 [16, 32, 128], P(None, ('member', 'region')), may hold values from -6 to 6
- obs_error: float32 [16, 32, 128], P(None, ('member', 'region')), may hold values from 0.5 to 4
- obs_index: int32 [16, 32, 128], P(None, ('member', 'region')), may hold values from 0 to 511
- obs_count: int32 [16, 32], P(None, ('member', 'region')), may hold values from 1 to 128
Outputs:
- analysis: float32 [12, 16, 32, 512], P('member', 'region')
Inputs may be any that keep to these rules, and one draw needn't show every extreme that they name: `obs_index`: value v names field v // (256) (0 SST, 1 SSH) at cell v mod (256) of the block, cells row-major. `obs_count`: slots below a block's count are observations; the others are padding and carry no weight.
All inputs are finite; a program needn't handle non-finite values.
Results may differ from a plain program's by a relative error of at most 0.0001.
Values sent between devices are 32-bit elements; how exact they have to be, the bound alone decides.
A program may use at most 64 MiB of HBM per device.

v0:
```python
import math

import jax
import jax.numpy as jnp
from jax import lax
from jax.sharding import PartitionSpec as P

SIDE = 16
NS_ITERS = 6


LOC_SCALE = 12.0
INFLATION_FACTOR = 1.1


def padded_2(cells, sides, width):
    for axis, dim in sides:
        count = lax.axis_size(axis)
        ends = count - 1
        head = lax.slice_in_dim(cells, 0, width, axis=dim)
        tail = lax.slice_in_dim(cells, cells.shape[dim] - width, cells.shape[dim], axis=dim)
        cells = jnp.concatenate(
            [
                lax.ppermute(tail, axis, [(i, (i + 1) % count) for i in range(ends)]),
                cells,
                lax.ppermute(head, axis, [((i + 1) % count, i) for i in range(ends)]),
            ],
            axis=dim,
        )
    return cells


def batch_product(left, right):
    return jnp.einsum("...ij,...jk->...ik", left, right, precision=lax.Precision.HIGHEST)


def observe(ensemble, obs_value, obs_error, obs_index, obs_count):
    ens_mean = jnp.mean(ensemble, axis=0)
    anomaly = ensemble - ens_mean
    slot_index = lax.broadcasted_iota(jnp.int32, obs_index.shape, 2)
    live_slot = jnp.where(slot_index < obs_count[:, :, None], 1.0, 0.0).astype(jnp.float32)
    root_weight = jnp.sqrt(live_slot / obs_error)
    value_count = anomaly.shape[3]
    value_ids = lax.broadcasted_iota(jnp.int32, (1, 1, 1, value_count), 3)
    selector = jnp.where(obs_index[:, :, :, None] == value_ids, 1.0, 0.0).astype(jnp.float32)
    seen_anom = jnp.einsum("rcov,krcv->rcko", selector, anomaly, precision=lax.Precision.HIGHEST)
    seen_mean = jnp.einsum("rcov,rcv->rco", selector, ens_mean, precision=lax.Precision.HIGHEST)
    rescaled_values = root_weight[:, :, None] * seen_anom
    innovation = root_weight * (obs_value - seen_mean)
    cell_index = obs_index % (SIDE * SIDE)
    rowpos = (cell_index // SIDE).astype(jnp.float32)
    column_position = (cell_index % SIDE).astype(jnp.float32)
    stacked = jnp.concatenate(
        [rescaled_values, innovation[:, :, None], rowpos[:, :, None], column_position[:, :, None]],
        axis=2,
    )
    return (anomaly, ens_mean, stacked)


def analyze(anomaly, ens_mean, padded):
    ensemble_members = anomaly.shape[0]
    row_count = anomaly.shape[1]
    col_count = anomaly.shape[2]
    pieces = []
    for row_step in range(3):
        for col_step in range(3):
            pieces.append(padded[row_step : row_step + row_count, col_step : col_step + col_count])
    nearby = jnp.stack(pieces, axis=2)
    rescaled_values = nearby[:, :, :, :ensemble_members]
    innovation = nearby[:, :, :, ensemble_members]
    rowpos = nearby[:, :, :, ensemble_members + 1]
    column_position = nearby[:, :, :, ensemble_members + 2]
    offset_index = jnp.arange(9, dtype=jnp.int32)
    offset_row = (offset_index // 3 - 1).astype(jnp.float32) * SIDE
    offset_col = (offset_index % 3 - 1).astype(jnp.float32) * SIDE
    half_side = SIDE // 2
    point_index = jnp.arange(4, dtype=jnp.int32)
    center_row = (point_index // 2).astype(jnp.float32) * half_side + (half_side - 1) * 0.5
    center_col = (point_index % 2).astype(jnp.float32) * half_side + (half_side - 1) * 0.5
    row_gap = offset_row[:, None] + rowpos
    col_gap = offset_col[:, None] + column_position
    distance = (row_gap[:, :, None] - center_row[:, None, None]) ** 2 + (
        col_gap[:, :, None] - center_col[:, None, None]
    ) ** 2
    locality = jnp.exp(-distance / (2.0 * LOC_SCALE * LOC_SCALE))
    weighted = locality[:, :, :, :, None, :] * rescaled_values[:, :, None]
    gramian_total = jnp.einsum(
        "rcpnko,rcnjo->rcpkj", weighted, rescaled_values, precision=lax.Precision.HIGHEST
    )
    drive_vec = jnp.einsum(
        "rcpnko,rcno->rcpk", weighted, innovation, precision=lax.Precision.HIGHEST
    )
    identity_matrix = jnp.eye(ensemble_members, dtype=jnp.float32)
    precision_matrix = gramian_total + (ensemble_members - 1) / INFLATION_FACTOR * identity_matrix
    norm_scale = jnp.sqrt(jnp.sum(precision_matrix * precision_matrix, axis=(3, 4), keepdims=True))
    root_iter = precision_matrix / norm_scale
    inv_iter = jnp.broadcast_to(identity_matrix, precision_matrix.shape)
    for sweep_index in range(NS_ITERS):
        ns_step = 1.5 * identity_matrix - 0.5 * batch_product(inv_iter, root_iter)
        root_iter = batch_product(root_iter, ns_step)
        inv_iter = batch_product(ns_step, inv_iter)
    inv_root = inv_iter / jnp.sqrt(norm_scale)
    half_way = jnp.einsum("rcpkj,rcpj->rcpk", inv_root, drive_vec, precision=lax.Precision.HIGHEST)
    mean_w = jnp.einsum("rcpkj,rcpj->rcpk", inv_root, half_way, precision=lax.Precision.HIGHEST)
    weights = mean_w[..., :, None] + math.sqrt(ensemble_members - 1) * inv_root
    point_weights = weights.reshape(row_count, col_count, 2, 2, ensemble_members, ensemble_members)
    shaped = anomaly.reshape(ensemble_members, row_count, col_count, 2, 2, half_side, 2, half_side)
    updated = jnp.einsum(
        "jrcvaybx,rcabjk->krcvaybx", shaped, point_weights, precision=lax.Precision.HIGHEST
    )
    return ens_mean[None] + updated.reshape(anomaly.shape)


def local(ensemble, obs_value, obs_error, obs_index, obs_count):
    members_dev = ensemble.shape[0]
    rows_dev = ensemble.shape[1]
    values_len = ensemble.shape[3]
    member_count = lax.axis_size("member")
    region_count = lax.axis_size("region")
    arrived = lax.all_to_all(
        ensemble[None], ("member", "region"), split_axis=3, concat_axis=0, tiled=True
    )
    col_dev = arrived.shape[3]
    grouped = arrived.reshape(
        member_count, region_count, members_dev, rows_dev, col_dev, values_len
    )
    by_block = jnp.transpose(grouped, (0, 2, 1, 3, 4, 5)).reshape(
        member_count * members_dev, region_count * rows_dev, col_dev, values_len
    )
    anomaly, ens_mean, stacked = observe(by_block, obs_value, obs_error, obs_index, obs_count)
    with_halo = padded_2(stacked, ((("member", "region"), 1),), 1)
    padded = jnp.pad(with_halo, ((1, 1), (0, 0), (0, 0), (0, 0)))
    row_span = anomaly.shape[1] // 8

    def one_group(turn_index, result):
        first_row_index = turn_index * row_span
        part_anom = lax.dynamic_slice_in_dim(anomaly, first_row_index, row_span, 1)
        part_mean = lax.dynamic_slice_in_dim(ens_mean, first_row_index, row_span, 0)
        part_pad = lax.dynamic_slice_in_dim(padded, first_row_index, row_span + 2, 0)
        return lax.dynamic_update_slice_in_dim(
            result, analyze(part_anom, part_mean, part_pad), first_row_index, 1
        )

    result = lax.fori_loop(0, 8, one_group, jnp.zeros_like(anomaly))
    col_dev = result.shape[2]
    regrouped = result.reshape(
        member_count, members_dev, region_count, rows_dev, col_dev, values_len
    )
    outgoing = jnp.transpose(regrouped, (0, 2, 1, 3, 4, 5)).reshape(
        member_count * region_count, members_dev, rows_dev, col_dev, values_len
    )
    returned = lax.all_to_all(
        outgoing, ("member", "region"), split_axis=0, concat_axis=3, tiled=True
    )
    return returned[0]


def solution(mesh):
    return jax.shard_map(
        local,
        mesh=mesh,
        in_specs=(
            P("member", "region", None, None),
            P(None, ("member", "region"), None),
            P(None, ("member", "region"), None),
            P(None, ("member", "region"), None),
            P(None, ("member", "region")),
        ),
        out_specs=P("member", "region", None, None),
        check_vma=False,
    )
```

profile of v0, /device:TPU:7, one launch (start us, length us, event | category | flops | bytes accessed | tf_op | source)
XLA Modules:
  0.0 169.8 jit_solution(10879895825682611400)
XLA Ops:
  0.0 2.1 %copy.99 = f32[3,2,32,512]{3,1,0,2:T(2,128)} copy(f32[3,2,32,512]{3,2,1,0:T(8,128)} %param.7) | data formatting | bytes 786432 | tf_op args[0]
  2.1 6.4 %all-to-all-start = ((f32[1,3,2,32,512]{4,2,1,0,3:T(2,128)}), f32[1,3,2,32,512]{4,2,1,0,3:T(2,128)S(1)}, u32[]{:S(2)}, u32[]{:S(2)}) async-start(f32[1,3,2,32,512]{4,2,1,0,3:T(2,128)} %bitcast.189), calls=%async_computation | async-start | bytes 786432 | tf_op jit(solution)/shard_map/all_to_all | solution.py:120
  8.5 11.7 %all-to-all-done = f32[1,3,2,32,512]{4,2,1,0,3:T(2,128)S(1)} async-done(((f32[1,3,2,32,512]{4,2,1,0,3:T(2,128)}), f32[1,3,2,32,512]{4,2,1,0,3:T(2,128)S(1)}, u32[]{:S(2)}, u32[]{:S(2)}) %all-to-all-start) | async-done | bytes 393248 | tf_op jit(solution)/shard_map/all_to_all | solution.py:120
  20.7 4.1 %fusion.36 = f32[16,1,128]{2,1,0:T(1,128)S(1)} fusion(f32[16,512,1]{1,2,0:T(1,128)S(1)} %reshape.524, s32[16,128]{1,0:T(8,128)S(1)} %bitcast.316), kind=kOutput, calls=%fused_computation.88 | convolution fusion | flops 14680064 | bytes 49152 | tf_op jit(solution)/shard_map/rcov,rcv->rco/dot_general | solution.py:47
  24.9 4.0 %fusion.49 = f32[16,1,12,128]{3,2,0,1:T(8,128)S(1)} fusion(s32[16,128]{1,0:T(8,128)S(1)} %bitcast.317, f32[12,16,512]{2,1,0:T(8,128)S(1)} %broadcast_subtract_fusion.1, f32[16,128]{1,0:T(8,128)S(1)} %get-tuple-element.195), kind=kOutput, calls=%fused_computation.100 | convolution fusion | flops 153116672 | bytes 507904 | tf_op jit(solution)/shard_map/rcov,krcv->rcko/dot_general | solution.py:46
  29.0 3.0 %collective-permute-start = (f32[16,1,15,128]{3,2,0,1:T(8,128)S(1)}, f32[16,1,15,128]{3,2,0,1:T(8,128)S(1)}, u32[]{:S(2)}, u32[]{:S(2)}) collective-permute-start(f32[16,1,15,128]{3,2,0,1:T(8,128)S(1)} %pad_maximum_fusion), channel_id=1, source_target_pairs={{0,1},{1,2},{2,3},{3,4},{4,5},{5,6},{6,7},{7,8},{8,9},{9,10},{10,1... | collective-permute-start | bytes 368648 | tf_op jit(solution)/shard_map/ppermute | solution.py:24
  31.9 2.5 %collective-permute-start.1 = (f32[16,1,15,128]{3,2,0,1:T(8,128)S(1)}, f32[16,1,15,128]{3,2,0,1:T(8,128)S(1)}, u32[]{:S(2)}, u32[]{:S(2)}) collective-permute-start(f32[16,1,15,128]{3,2,0,1:T(8,128)S(1)} %pad_maximum_fusion), channel_id=1, source_target_pairs={{1,0},{2,1},{3,2},{4,3},{5,4},{6,5},{7,6},{8,7},{9,8},{10,9},{11,1... | collective-permute-start | bytes 368648 | tf_op jit(solution)/shard_map/ppermute | solution.py:26
  35.5 3.7 %collective-permute-done.1 = f32[16,1,15,128]{3,2,0,1:T(8,128)S(1)} collective-permute-done((f32[16,1,15,128]{3,2,0,1:T(8,128)S(1)}, f32[16,1,15,128]{3,2,0,1:T(8,128)S(1)}, u32[]{:S(2)}, u32[]{:S(2)}) %collective-permute-start.1) | collective-permute-done | bytes 122912 | tf_op jit(solution)/shard_map/ppermute | solution.py:26
  39.3 109.6 %while.16 = (s32[]{:T(128)}, f32[12,16,1,512]{3,1,0,2:T(8,128)S(1)}, f32[16,1,512]{2,0,1:T(8,128)S(1)}, f32[18,3,15,128]{3,2,0,1:T(8,128)S(1)}, f32[12,16,1,512]...) while((s32[]{:T(128)}, ...), condition=%wide.region_3.4_spmd, body=%wide.region_1.3_spmd.sunk | while | flops 22196300 | bytes 2025700 | solution.py:144
  39.8 2.4 %convolution_bitcast_fusion.7 = f32[2,4,12,1]{2,3,1,0:T(1,128)S(1)} fusion(f32[2,9,12,128]{3,2,1,0:T(8,128)S(1)} %slice_bitcast_fusion.2, f32[2,4,9,128]{3,2,1,0:T(8,128)S(1)} %multiply_exponential_fusion.2, f32[2,9,128,1,1]{2,0,1,3,4:T(2,128)S(1)} %bitcast.308), kind=kOutput, calls=%fused_computation.17.clone.1 | convolution fusion | flops 1437696 | bytes 157056 | tf_op jit(solution)/shard_map/while/body/eval_jaxpr/rcpnko,rcno->rcpk/dot_general | solution.py:90
  48.3 2.1 %convolution_bitcast_fusion.9 = f32[12,2,1,2,2,8,2,8]{0,7,5,3,6,4,1,2:T(8,128)S(1)} fusion(f32[2,2,2,12,12,1,1]{4,3,6,5,2,1,0:T(8,128)S(1)} %bitcast.300, f32[12,2,2,2,8,2,8]{6,5,4,3,2,1,0:T(2,128)S(1)} %reshape.527), kind=kOutput, calls=%fused_computation.clone.1 | convolution fusion | flops 1769472 | bytes 102912 | tf_op jit(solution)/shard_map/while/body/eval_jaxpr/jrcvaybx,rcabjk->krcvaybx/dot_general | solution.py:108
  50.4 1.4 copy.115
  53.5 2.4 %convolution_bitcast_fusion.7 = f32[2,4,12,1]{2,3,1,0:T(1,128)S(1)} fusion(f32[2,9,12,128]{3,2,1,0:T(8,128)S(1)} %slice_bitcast_fusion.2, f32[2,4,9,128]{3,2,1,0:T(8,128)S(1)} %multiply_exponential_fusion.2, f32[2,9,128,1,1]{2,0,1,3,4:T(2,128)S(1)} %bitcast.308), kind=kOutput, calls=%fused_computation.17.clone.1 | convolution fusion | flops 1437696 | bytes 157056 | tf_op jit(solution)/shard_map/while/body/eval_jaxpr/rcpnko,rcno->rcpk/dot_general | solution.py:90
  62.0 2.1 %convolution_bitcast_fusion.9 = f32[12,2,1,2,2,8,2,8]{0,7,5,3,6,4,1,2:T(8,128)S(1)} fusion(f32[2,2,2,12,12,1,1]{4,3,6,5,2,1,0:T(8,128)S(1)} %bitcast.300, f32[12,2,2,2,8,2,8]{6,5,4,3,2,1,0:T(2,128)S(1)} %reshape.527), kind=kOutput, calls=%fused_computation.clone.1 | convolution fusion | flops 1769472 | bytes 102912 | tf_op jit(solution)/shard_map/while/body/eval_jaxpr/jrcvaybx,rcabjk->krcvaybx/dot_general | solution.py:108
  64.1 1.4 copy.115
  67.2 2.4 %convolution_bitcast_fusion.7 = f32[2,4,12,1]{2,3,1,0:T(1,128)S(1)} fusion(f32[2,9,12,128]{3,2,1,0:T(8,128)S(1)} %slice_bitcast_fusion.2, f32[2,4,9,128]{3,2,1,0:T(8,128)S(1)} %multiply_exponential_fusion.2, f32[2,9,128,1,1]{2,0,1,3,4:T(2,128)S(1)} %bitcast.308), kind=kOutput, calls=%fused_computation.17.clone.1 | convolution fusion | flops 1437696 | bytes 157056 | tf_op jit(solution)/shard_map/while/body/eval_jaxpr/rcpnko,rcno->rcpk/dot_general | solution.py:90
  75.7 2.1 %convolution_bitcast_fusion.9 = f32[12,2,1,2,2,8,2,8]{0,7,5,3,6,4,1,2:T(8,128)S(1)} fusion(f32[2,2,2,12,12,1,1]{4,3,6,5,2,1,0:T(8,128)S(1)} %bitcast.300, f32[12,2,2,2,8,2,8]{6,5,4,3,2,1,0:T(2,128)S(1)} %reshape.527), kind=kOutput, calls=%fused_computation.clone.1 | convolution fusion | flops 1769472 | bytes 102912 | tf_op jit(solution)/shard_map/while/body/eval_jaxpr/jrcvaybx,rcabjk->krcvaybx/dot_general | solution.py:108
  77.8 1.4 copy.115
  80.9 2.4 %convolution_bitcast_fusion.7 = f32[2,4,12,1]{2,3,1,0:T(1,128)S(1)} fusion(f32[2,9,12,128]{3,2,1,0:T(8,128)S(1)} %slice_bitcast_fusion.2, f32[2,4,9,128]{3,2,1,0:T(8,128)S(1)} %multiply_exponential_fusion.2, f32[2,9,128,1,1]{2,0,1,3,4:T(2,128)S(1)} %bitcast.308), kind=kOutput, calls=%fused_computation.17.clone.1 | convolution fusion | flops 1437696 | bytes 157056 | tf_op jit(solution)/shard_map/while/body/eval_jaxpr/rcpnko,rcno->rcpk/dot_general | solution.py:90
  89.4 2.1 %convolution_bitcast_fusion.9 = f32[12,2,1,2,2,8,2,8]{0,7,5,3,6,4,1,2:T(8,128)S(1)} fusion(f32[2,2,2,12,12,1,1]{4,3,6,5,2,1,0:T(8,128)S(1)} %bitcast.300, f32[12,2,2,2,8,2,8]{6,5,4,3,2,1,0:T(2,128)S(1)} %reshape.527), kind=kOutput, calls=%fused_computation.clone.1 | convolution fusion | flops 1769472 | bytes 102912 | tf_op jit(solution)/shard_map/while/body/eval_jaxpr/jrcvaybx,rcabjk->krcvaybx/dot_general | solution.py:108
  91.5 1.4 copy.115
  94.6 2.4 %convolution_bitcast_fusion.7 = f32[2,4,12,1]{2,3,1,0:T(1,128)S(1)} fusion(f32[2,9,12,128]{3,2,1,0:T(8,128)S(1)} %slice_bitcast_fusion.2, f32[2,4,9,128]{3,2,1,0:T(8,128)S(1)} %multiply_exponential_fusion.2, f32[2,9,128,1,1]{2,0,1,3,4:T(2,128)S(1)} %bitcast.308), kind=kOutput, calls=%fused_computation.17.clone.1 | convolution fusion | flops 1437696 | bytes 157056 | tf_op jit(solution)/shard_map/while/body/eval_jaxpr/rcpnko,rcno->rcpk/dot_general | solution.py:90
  103.1 2.1 %convolution_bitcast_fusion.9 = f32[12,2,1,2,2,8,2,8]{0,7,5,3,6,4,1,2:T(8,128)S(1)} fusion(f32[2,2,2,12,12,1,1]{4,3,6,5,2,1,0:T(8,128)S(1)} %bitcast.300, f32[12,2,2,2,8,2,8]{6,5,4,3,2,1,0:T(2,128)S(1)} %reshape.527), kind=kOutput, calls=%fused_computation.clone.1 | convolution fusion | flops 1769472 | bytes 102912 | tf_op jit(solution)/shard_map/while/body/eval_jaxpr/jrcvaybx,rcabjk->krcvaybx/dot_general | solution.py:108
  105.2 1.4 copy.115
  108.3 2.4 %convolution_bitcast_fusion.7 = f32[2,4,12,1]{2,3,1,0:T(1,128)S(1)} fusion(f32[2,9,12,128]{3,2,1,0:T(8,128)S(1)} %slice_bitcast_fusion.2, f32[2,4,9,128]{3,2,1,0:T(8,128)S(1)} %multiply_exponential_fusion.2, f32[2,9,128,1,1]{2,0,1,3,4:T(2,128)S(1)} %bitcast.308), kind=kOutput, calls=%fused_computation.17.clone.1 | convolution fusion | flops 1437696 | bytes 157056 | tf_op jit(solution)/shard_map/while/body/eval_jaxpr/rcpnko,rcno->rcpk/dot_general | solution.py:90
  116.8 2.1 %convolution_bitcast_fusion.9 = f32[12,2,1,2,2,8,2,8]{0,7,5,3,6,4,1,2:T(8,128)S(1)} fusion(f32[2,2,2,12,12,1,1]{4,3,6,5,2,1,0:T(8,128)S(1)} %bitcast.300, f32[12,2,2,2,8,2,8]{6,5,4,3,2,1,0:T(2,128)S(1)} %reshape.527), kind=kOutput, calls=%fused_computation.clone.1 | convolution fusion | flops 1769472 | bytes 102912 | tf_op jit(solution)/shard_map/while/body/eval_jaxpr/jrcvaybx,rcabjk->krcvaybx/dot_general | solution.py:108
  118.9 1.4 copy.115
  122.0 2.4 %convolution_bitcast_fusion.7 = f32[2,4,12,1]{2,3,1,0:T(1,128)S(1)} fusion(f32[2,9,12,128]{3,2,1,0:T(8,128)S(1)} %slice_bitcast_fusion.2, f32[2,4,9,128]{3,2,1,0:T(8,128)S(1)} %multiply_exponential_fusion.2, f32[2,9,128,1,1]{2,0,1,3,4:T(2,128)S(1)} %bitcast.308), kind=kOutput, calls=%fused_computation.17.clone.1 | convolution fusion | flops 1437696 | bytes 157056 | tf_op jit(solution)/shard_map/while/body/eval_jaxpr/rcpnko,rcno->rcpk/dot_general | solution.py:90
  130.5 2.1 %convolution_bitcast_fusion.9 = f32[12,2,1,2,2,8,2,8]{0,7,5,3,6,4,1,2:T(8,128)S(1)} fusion(f32[2,2,2,12,12,1,1]{4,3,6,5,2,1,0:T(8,128)S(1)} %bitcast.300, f32[12,2,2,2,8,2,8]{6,5,4,3,2,1,0:T(2,128)S(1)} %reshape.527), kind=kOutput, calls=%fused_computation.clone.1 | convolution fusion | flops 1769472 | bytes 102912 | tf_op jit(solution)/shard_map/while/body/eval_jaxpr/jrcvaybx,rcabjk->krcvaybx/dot_general | solution.py:108
  135.7 2.4 %convolution_bitcast_fusion.7 = f32[2,4,12,1]{2,3,1,0:T(1,128)S(1)} fusion(f32[2,9,12,128]{3,2,1,0:T(8,128)S(1)} %slice_bitcast_fusion.2, f32[2,4,9,128]{3,2,1,0:T(8,128)S(1)} %multiply_exponential_fusion.2, f32[2,9,128,1,1]{2,0,1,3,4:T(2,128)S(1)} %bitcast.308), kind=kOutput, calls=%fused_computation.17.clone.1 | convolution fusion | flops 1437696 | bytes 157056 | tf_op jit(solution)/shard_map/while/body/eval_jaxpr/rcpnko,rcno->rcpk/dot_general | solution.py:90
  144.2 2.1 %convolution_bitcast_fusion.9 = f32[12,2,1,2,2,8,2,8]{0,7,5,3,6,4,1,2:T(8,128)S(1)} fusion(f32[2,2,2,12,12,1,1]{4,3,6,5,2,1,0:T(8,128)S(1)} %bitcast.300, f32[12,2,2,2,8,2,8]{6,5,4,3,2,1,0:T(2,128)S(1)} %reshape.527), kind=kOutput, calls=%fused_computation.clone.1 | convolution fusion | flops 1769472 | bytes 102912 | tf_op jit(solution)/shard_map/while/body/eval_jaxpr/jrcvaybx,rcabjk->krcvaybx/dot_general | solution.py:108
  149.2 19.8 %all_to_all.30 = f32[32,3,2,1,512]{4,2,1,3,0:T(2,128)S(1)} all-to-all(f32[32,3,2,1,512]{4,2,1,3,0:T(2,128)S(1)} %bitcast.305), channel_id=1, replica_groups=mesh['member'=4,'region'=8] {'member','region'}, dimensions={0} | all-to-all | bytes 786432 | tf_op jit(solution)/shard_map/all_to_all | solution.py:152
  (421 shorter events, 65.5 us)
Async XLA Ops:
  0.0 8.4 %copy-start = (s32[16,1,128]{2,1,0:T(1,128)S(1)}, s32[16,1,128]{2,1,0:T(1,128)}, u32[]{:S(2)}) copy-start(s32[16,1,128]{2,1,0:T(1,128)} %param.10) | copy-start | bytes 24580
  2.1 18.1 %all-to-all-start = ((f32[1,3,2,32,512]{4,2,1,0,3:T(2,128)}), f32[1,3,2,32,512]{4,2,1,0,3:T(2,128)S(1)}, u32[]{:S(2)}, u32[]{:S(2)}) async-start(f32[1,3,2,32,512]{4,2,1,0,3:T(2,128)} %bitcast.189), calls=%async_computation | async-start | bytes 786432 | tf_op jit(solution)/shard_map/all_to_all | solution.py:120
  20.7 4.1 %copy-start.1 = (f32[16,1,128]{2,1,0:T(1,128)S(1)}, f32[16,1,128]{2,1,0:T(1,128)}, u32[]{:S(2)}) copy-start(f32[16,1,128]{2,1,0:T(1,128)} %param.9) | copy-start | bytes 24580
  20.7 4.1 %copy-start.2 = (f32[16,1,128]{2,1,0:T(1,128)S(1)}, f32[16,1,128]{2,1,0:T(1,128)}, u32[]{:S(2)}) copy-start(f32[16,1,128]{2,1,0:T(1,128)} %param.8) | copy-start | bytes 24580
  20.7 4.1 %copy-start.3 = (s32[16,1]{0,1:T(1,128)S(1)}, s32[16,1]{0,1:T(1,128)}, u32[]{:S(2)}) copy-start(s32[16,1]{0,1:T(1,128)} %param.11) | copy-start | bytes 196
  29.0 6.6 %collective-permute-start = (f32[16,1,15,128]{3,2,0,1:T(8,128)S(1)}, f32[16,1,15,128]{3,2,0,1:T(8,128)S(1)}, u32[]{:S(2)}, u32[]{:S(2)}) collective-permute-start(f32[16,1,15,128]{3,2,0,1:T(8,128)S(1)} %pad_maximum_fusion), channel_id=1, source_target_pairs={{0,1},{1,2},{2,3},{3,4},{4,5},{5,6},{6,7},{7,8},{8,9},{9,10},{10,1... | collective-permute-start | bytes 368648 | tf_op jit(solution)/shard_map/ppermute | solution.py:24
  31.9 7.2 %collective-permute-start.1 = (f32[16,1,15,128]{3,2,0,1:T(8,128)S(1)}, f32[16,1,15,128]{3,2,0,1:T(8,128)S(1)}, u32[]{:S(2)}, u32[]{:S(2)}) collective-permute-start(f32[16,1,15,128]{3,2,0,1:T(8,128)S(1)} %pad_maximum_fusion), channel_id=1, source_target_pairs={{1,0},{2,1},{3,2},{4,3},{5,4},{6,5},{7,6},{8,7},{9,8},{10,9},{11,1... | collective-permute-start | bytes 368648 | tf_op jit(solution)/shard_map/ppermute | solution.py:26
where the time goes:
time: 173 us; the launch traced here: 170 us
  matrix products  79.8 us (46%)
  local copies, waits for them, and re-layouts  35.4 us (20%)
  blocking collectives  19.8 us (11%)
  waiting for transfers between devices  16.1 us (9%)
  starting transfers between devices  11.8 us (7%)
  other arithmetic  3.63 us (2%)
  loops' own time  3.01 us (2%)
    dot_general x136, matrix products, batch_product(): jnp.einsum('...ij,...jk->...ik', left, right, precision=lax.Precision.HIG...  26.5 us
    all_to_all x1, blocking collectives, local(): lax.all_to_all(outgoing, ('member', 'region'), split_axis=0, concat_axis=...  19.8 us
    dot_general x8, matrix products, analyze(): jnp.einsum('rcpnko,rcno->rcpk', weighted, innovation, precision=lax.Preci...  19 us
    dot_general x8, matrix products, analyze(): jnp.einsum('jrcvaybx,rcabjk->krcvaybx', shaped, point_weights, precision=...  16.6 us
    all_to_all x1, waiting for transfers between devices, local(): lax.all_to_all(ensemble[None], ('member', 'region'), split_axis=3, concat...  11.7 us
    transpose x8, local copies, waits for them, and re-layouts, analyze(): jnp.einsum('jrcvaybx,rcabjk->krcvaybx', shaped, point_weights, precision=...  11.2 us
    another operation x8, local copies, waits for them, and re-layouts  9.76 us
    reshape x8, local copies, waits for them, and re-layouts, analyze(): return ens_mean[None] + updated.reshape(anomaly.shape)  9.01 us
  transfers between devices with their start and end apart: 3, of which 3 were waited for; matrix products, arithmetic and copies ran while one was open for 0% of the time, Pallas kernels for 0%

commit v1 on v0

v1 whole, which is shorter than its diff:
```python
import functools
import math

import jax
import jax.numpy as jnp
from jax import lax
from jax.experimental import pallas as pl
from jax.experimental.pallas import tpu as pltpu
from jax.sharding import PartitionSpec as P

SIDE = 16
CELLS = SIDE * SIDE
HALF = SIDE // 2
LANES = 128
NS_ITERS = 6
LOC_SCALE = 12.0
INFLATION_FACTOR = 1.1
MESH = pl.DeviceIdType.MESH
NT = (((1,), (1,)), ((), ()))


def up_to(value, step):
    return -(-value // step) * step


def split(values):
    high = values.astype(jnp.bfloat16)
    low = (values - high.astype(jnp.float32)).astype(jnp.bfloat16)
    return high, low


def kernel(
    dims,
    ens_ref, value_ref, error_ref, index_ref, count_ref, out_ref,
    ens, pack, obs, mean, slots, place, loc, qhi, qlo, acc, side,
    row_in, side_in, prec, root, inv, step, small, weights, outgoing,
    ens_send, ens_recv, obs_send, obs_recv, halo_send, halo_recv, out_send, out_recv, local_sem,
):
    M, G, K, R, C, V, O, J, QP = dims
    members = M * K
    m = lax.axis_index("member")
    g = lax.axis_index("region")
    pack_rows = pack.shape[0] // G
    ts = 2 * (R + 2)
    targets = 4 * C * (R + 2)
    f32 = jnp.float32

    barrier = pltpu.get_barrier_semaphore()
    for off in range(1, M):
        pl.semaphore_signal(barrier, inc=1, device_id=(lax.rem(m + off, M), g), device_id_type=MESH)
    for off in range(1, G):
        pl.semaphore_signal(barrier, inc=1, device_id=(m, lax.rem(g + off, G)), device_id_type=MESH)
    near = {}
    for dm in (-1, 0, 1):
        for dg in (-1, 0, 1):
            if dm == 0 and dg == 0:
                continue
            ok = jnp.bool_(True)
            if dm:
                ok = jnp.logical_and(ok, m > 0 if dm < 0 else m < M - 1)
            if dg:
                ok = jnp.logical_and(ok, g > 0 if dg < 0 else g < G - 1)
            near[dm, dg] = ok
            if dm and dg:
                @pl.when(ok)
                def _():
                    pl.semaphore_signal(barrier, inc=1, device_id=(m + dm, g + dg), device_id_type=MESH)

    own_ens = pltpu.make_async_copy(
        ens_ref.at[:, :, pl.ds(pl.multiple_of(m * C, C), C), :], ens.at[pl.ds(m * K, K)], local_sem.at[0]
    )
    own_ens.start()
    slot = lax.broadcasted_iota(jnp.int32, (G * R, O), 1)
    slot_row = lax.broadcasted_iota(jnp.int32, (G * R, O), 0)
    count = jnp.zeros((G * R, O), jnp.int32)
    for d in range(G * R):
        count = jnp.where(slot_row == d, count_ref[0, d], count)
    live = jnp.where(slot < count, 1.0, 0.0).astype(f32)
    weight = jnp.sqrt(live / error_ref[...])
    value = value_ref[...]
    index_f = index_ref[...].astype(f32)
    for d in range(G):
        base = d * pack_rows
        pack[base : base + R, :] = weight[d * R : (d + 1) * R]
        pack[base + R : base + 2 * R, :] = value[d * R : (d + 1) * R]
        pack[base + 2 * R : base + 3 * R, :] = index_f[d * R : (d + 1) * R]
        if pack_rows > 3 * R:
            pack[base + 3 * R : base + pack_rows, :] = jnp.zeros((pack_rows - 3 * R, O), f32)
    if QP > members * J:
        qhi[members * J :, :] = jnp.zeros((QP - members * J, qhi.shape[1]), jnp.bfloat16)
        qlo[members * J :, :] = jnp.zeros((QP - members * J, qlo.shape[1]), jnp.bfloat16)

    sides = jnp.where(m > 0, 1, 0) + jnp.where(m < M - 1, 1, 0)
    ends = jnp.where(g > 0, 1, 0) + jnp.where(g < G - 1, 1, 0)
    pl.semaphore_wait(barrier, M - 1 + G - 1 + sides * ends)

    sends = []
    for off in range(1, M):
        to = lax.rem(m + off, M)
        copy = pltpu.make_async_remote_copy(
            src_ref=ens_ref.at[:, :, pl.ds(pl.multiple_of(to * C, C), C), :],
            dst_ref=ens.at[pl.ds(m * K, K)],
            send_sem=ens_send.at[off], recv_sem=ens_recv.at[off],
            device_id=(to, g), device_id_type=MESH,
        )
        copy.start()
        sends.append(copy)
    own_row = pl.ds(pl.multiple_of(g * pack_rows, pack_rows), pack_rows)
    own_obs = pltpu.make_async_copy(pack.at[own_row], obs.at[own_row], local_sem.at[1])
    own_obs.start()
    for off in range(1, G):
        to = lax.rem(g + off, G)
        copy = pltpu.make_async_remote_copy(
            src_ref=pack.at[pl.ds(pl.multiple_of(to * pack_rows, pack_rows), pack_rows)],
            dst_ref=obs.at[own_row],
            send_sem=obs_send.at[off], recv_sem=obs_recv.at[off],
            device_id=(m, to), device_id_type=MESH,
        )
        copy.start()
        sends.append(copy)
    own_ens.wait()
    own_obs.wait()
    for off in range(1, M):
        came = lax.rem(m + M - off, M)
        pltpu.make_async_remote_copy(
            src_ref=ens_ref.at[:, :, pl.ds(pl.multiple_of(m * C, C), C), :],
            dst_ref=ens.at[pl.ds(came * K, K)],
            send_sem=ens_send.at[off], recv_sem=ens_recv.at[off],
            device_id=(came, g), device_id_type=MESH,
        ).wait_recv()
    for off in range(1, G):
        came = lax.rem(g + G - off, G)
        pltpu.make_async_remote_copy(
            src_ref=pack.at[own_row],
            dst_ref=obs.at[pl.ds(pl.multiple_of(came * pack_rows, pack_rows), pack_rows)],
            send_sem=obs_send.at[off], recv_sem=obs_recv.at[off],
            device_id=(m, came), device_id_type=MESH,
        ).wait_recv()

    tiles = V // LANES
    for i in range(R):
        wgt = obs[pl.ds(i, C, stride=pack_rows), :]
        val = obs[pl.ds(R + i, C, stride=pack_rows), :]
        idx = obs[pl.ds(2 * R + i, C, stride=pack_rows), :].astype(jnp.int32)
        lane = idx & (LANES - 1)
        tile = idx >> 7
        cell = idx & (CELLS - 1)
        place[2 * i] = (cell >> 4).astype(f32)
        place[2 * i + 1] = (cell & (SIDE - 1)).astype(f32)

        def seen(rows):
            got = jnp.take_along_axis(rows[:, :LANES], lane, axis=1)
            for t in range(1, tiles):
                more = jnp.take_along_axis(rows[:, t * LANES : (t + 1) * LANES], lane, axis=1)
                got = jnp.where(tile == t, more, got)
            return got

        total = ens[0, i]
        for k in range(1, members):
            total = total + ens[k, i]
        avg = total * (1.0 / members)
        mean[i] = avg
        seen_mean = seen(avg)
        base = i * J * C
        for k in range(members):
            slots[base + k * C : base + (k + 1) * C, :] = wgt * (seen(ens[k, i]) - seen_mean)
        slots[base + members * C : base + (members + 1) * C, :] = wgt * (val - seen_mean)
        if J > members + 1:
            slots[base + (members + 1) * C : base + J * C, :] = jnp.zeros(((J - members - 1) * C, O), f32)

    scale = -1.0 / (2.0 * LOC_SCALE * LOC_SCALE)
    middle = (HALF - 1) * 0.5
    t_id = lax.broadcasted_iota(jnp.int32, (ts, O), 0)
    t_row = t_id >> 1
    t_mid = (t_id & 1).astype(f32) * HALF + middle
    col = lax.broadcasted_iota(jnp.int32, (C, O), 0)
    edges = {0: [None] * R, 1: [None] * R}
    for c in range(C):
        for i in range(R):
            at = (c * R + i) * O
            here = slots[pl.ds(i * J * C + c, J, stride=C), :]
            prod = jnp.concatenate([here[k : k + 1] * here for k in range(members)], axis=0)
            high, low = split(prod)
            qhi[0 : members * J, at : at + O] = high
            qlo[0 : members * J, at : at + O] = low
            y = place[2 * i, c : c + 1, :]
            x = place[2 * i + 1, c : c + 1, :]
            row_off = i + 1 - t_row
            dy = (row_off * SIDE).astype(f32) + y - t_mid
            ly = jnp.where(jnp.abs(row_off) <= 1, jnp.exp(dy * dy * scale), 0.0)
            col_off = c - col
            lx = []
            for pc in range(2):
                dx = (col_off * SIDE).astype(f32) + x - (pc * HALF + middle)
                lx.append(jnp.where(jnp.abs(col_off) <= 1, jnp.exp(dx * dx * scale), 0.0))
            grid = jnp.concatenate([ly[s : s + 1] * lx[pc] for s in range(ts) for pc in range(2)], axis=0)
            high, low = split(grid)
            loc[0:targets, at : at + O] = high
            loc[targets : 2 * targets, at : at + O] = low
            for which, away, at_col in ((0, 1, 0), (1, -1, C - 1)):
                if c == at_col:
                    parts = []
                    for pc in range(2):
                        dx = away * SIDE + x - (pc * HALF + middle)
                        parts.append(ly * jnp.exp(dx * dx * scale))
                    edges[which][i] = jnp.concatenate(parts, axis=0)

    def dot(left, right):
        return lax.dot_general(left, right, NT, preferred_element_type=f32)

    for which, first in ((0, 0), (1, (C - 1) * R * O)):
        high, low = split(jnp.concatenate(edges[which], axis=1))
        hq = qhi[:, first : first + R * O]
        side[which] = dot(high, hq) + dot(low, hq) + dot(high, qlo[:, first : first + R * O])
    both = dot(loc[...], qhi[...])
    acc[...] = both[:targets] + both[targets:] + dot(loc[0:targets, :], qlo[...])

    rows = 4 * C
    plans = []
    for n, (dm, dg) in enumerate(near):
        if dm == 0:
            first = 0 if dg < 0 else (R + 1) * rows
            src = acc.at[first : first + rows]
            dst = row_in.at[0 if dg < 0 else 1]
        else:
            src = side.at[0 if dm < 0 else 1]
            dst = side_in.at[(0 if dm < 0 else 3) + dg + 1]
        plans.append((dm, dg, src, dst, n))
    for dm, dg, src, dst, n in plans:
        @pl.when(near[dm, dg])
        def _():
            pltpu.make_async_remote_copy(
                src_ref=src, dst_ref=dst, send_sem=halo_send.at[n], recv_sem=halo_recv.at[n],
                device_id=(m + dm, g + dg), device_id_type=MESH,
            ).start()
    for dm, dg, src, dst, n in plans:
        @pl.when(near[-dm, -dg])
        def _():
            pltpu.make_async_remote_copy(
                src_ref=src, dst_ref=dst, send_sem=halo_send.at[n], recv_sem=halo_recv.at[n],
                device_id=(m - dm, g - dg), device_id_type=MESH,
            ).wait_recv()

        @pl.when(jnp.logical_not(near[-dm, -dg]))
        def _():
            dst[...] = jnp.zeros(dst.shape, f32)

    sub = lax.broadcasted_iota(jnp.int32, (C, QP), 0)
    own = R * rows
    for i in range(R):
        for pr in range(2):
            for pc in range(2):
                first = (i * 4 + pr * 2 + pc) * C
                block = acc[rows + first : rows + first + C, :]
                if i == R - 1:
                    block = block + row_in[0, (pr * 2 + pc) * C : (pr * 2 + pc + 1) * C, :]
                if i == 0:
                    block = block + row_in[1, (pr * 2 + pc) * C : (pr * 2 + pc + 1) * C, :]
                for base, at_col in ((0, C - 1), (3, 0)):
                    def pick(dg, t):
                        place_in = pc * ts + t * 2 + pr
                        return side_in[base + dg + 1, place_in : place_in + 1, :]

                    line = pick(0, i + 1)
                    if i == R - 1:
                        line = line + pick(-1, 0)
                    if i == 0:
                        line = line + pick(1, R + 1)
                    block = block + jnp.where(sub == at_col, line, 0.0)
                prec[first : first + C, :] = block
    width = prec.shape[0]
    if width > own:
        prec[own:, :] = jnp.zeros((width - own, QP), f32)

    flat = jnp.transpose(prec[...])
    j_id = lax.broadcasted_iota(jnp.int32, (J, width), 0)
    eye = [jnp.where(j_id == k, 1.0, 0.0).astype(f32) for k in range(members)]
    drive = []
    mats = []
    squares = None
    for k in range(members):
        line = flat[k * J : (k + 1) * J]
        drive.append(line[members : members + 1])
        mat = jnp.where(j_id < members, line, 0.0) + ((members - 1) / INFLATION_FACTOR) * eye[k]
        mats.append(mat)
        squares = mat * mat if squares is None else squares + mat * mat
    norm = jnp.sqrt(jnp.sum(squares, axis=0, keepdims=True))
    for k in range(members):
        start = mats[k] / norm
        first_m = 1.5 * eye[k] - 0.5 * start
        root[k] = start
        step[k] = first_m
        inv[k] = first_m

    def times(left, k, right):
        out = left[k, 0:1, :] * right[0]
        for i in range(1, members):
            out = out + left[k, i : i + 1, :] * right[i]
        return out

    def apply(*lefts):
        right = [step[i] for i in range(members)]
        for k in range(members):
            for left in lefts:
                left[k] = times(left, k, right)

    def next_step():
        right = [root[i] for i in range(members)]
        for k in range(members):
            step[k] = 1.5 * jnp.where(j_id == k, 1.0, 0.0) - 0.5 * times(inv, k, right)

    apply(root)

    def sweep(_, carry):
        next_step()
        apply(root, inv)
        return carry

    lax.fori_loop(0, NS_ITERS - 2, sweep, 0)
    next_step()
    apply(inv)
    shrink = 1.0 / jnp.sqrt(norm)
    inv_root = [inv[k] * shrink for k in range(members)]
    half_way = drive[0] * inv_root[0]
    for i in range(1, members):
        half_way = half_way + drive[i] * inv_root[i]
    small[0] = half_way
    mean_w = small[0, 0:1, :] * inv_root[0]
    for i in range(1, members):
        mean_w = mean_w + small[0, i : i + 1, :] * inv_root[i]
    small[1] = mean_w
    for j in range(members):
        weights[j * J : (j + 1) * J, :] = small[1, j : j + 1, :] + math.sqrt(members - 1) * inv_root[j]
    if QP > members * J:
        weights[members * J :, :] = jnp.zeros((QP - members * J, width), f32)
    prec[...] = jnp.transpose(weights[...])

    fields = V // CELLS
    band = HALF * SIDE
    left_half = (lax.broadcasted_iota(jnp.int32, (C, band), 1) & (SIDE - 1)) < HALF
    for dest in range(M):
        for i in range(R):
            for h in range(2):
                first = (i * 4 + 2 * h) * C
                west = prec[first : first + C, :]
                east = prec[first + C : first + 2 * C, :]
                lanes = [f * CELLS + h * band for f in range(fields)]
                avgs = [mean[i, :, a : a + band] for a in lanes]
                outs = [[avgs[f] for f in range(fields)] for _ in range(K)]
                for j in range(members):
                    anoms = [ens[j, i, :, a : a + band] - avgs[f] for f, a in enumerate(lanes)]
                    for kk in range(K):
                        q = j * J + dest * K + kk
                        w = jnp.where(
                            left_half,
                            jnp.broadcast_to(west[:, q : q + 1], (C, band)),
                            jnp.broadcast_to(east[:, q : q + 1], (C, band)),
                        )
                        for f in range(fields):
                            outs[kk][f] = outs[kk][f] + anoms[f] * w
                for kk in range(K):
                    for f, a in enumerate(lanes):
                        outgoing[dest * K + kk, i, :, a : a + band] = outs[kk][f]
        away = lax.rem(dest - m + M, M)
        target = out_ref.at[:, :, pl.ds(pl.multiple_of(m * C, C), C), :]

        @pl.when(away != 0)
        def _():
            pltpu.make_async_remote_copy(
                src_ref=outgoing.at[dest * K : (dest + 1) * K], dst_ref=target,
                send_sem=out_send.at[away], recv_sem=out_recv.at[away],
                device_id=(dest, g), device_id_type=MESH,
            ).start()

        @pl.when(away == 0)
        def _():
            pltpu.make_async_copy(outgoing.at[dest * K : (dest + 1) * K], target, local_sem.at[2]).start()

    for copy in sends:
        copy.wait_send()
    for dm, dg, src, dst, n in plans:
        @pl.when(near[dm, dg])
        def _():
            pltpu.make_async_remote_copy(
                src_ref=src, dst_ref=dst, send_sem=halo_send.at[n], recv_sem=halo_recv.at[n],
                device_id=(m + dm, g + dg), device_id_type=MESH,
            ).wait_send()
    pltpu.make_async_copy(
        outgoing.at[pl.ds(m * K, K)], out_ref.at[:, :, pl.ds(pl.multiple_of(m * C, C), C), :], local_sem.at[2]
    ).wait()
    for off in range(1, M):
        to = lax.rem(m + off, M)
        came = lax.rem(m + M - off, M)
        pltpu.make_async_remote_copy(
            src_ref=outgoing.at[pl.ds(to * K, K)],
            dst_ref=out_ref.at[:, :, pl.ds(pl.multiple_of(came * C, C), C), :],
            send_sem=out_send.at[off], recv_sem=out_recv.at[off],
            device_id=(to, g), device_id_type=MESH,
        ).wait()


def local(M, G, ensemble, obs_value, obs_error, obs_index, obs_count):
    K, R, cols, V = ensemble.shape
    O = obs_value.shape[2]
    C = cols // M
    members = M * K
    J = up_to(members + 1, 8)
    QP = up_to(members * J, LANES)
    slots_all = R * C * O
    targets = 4 * C * (R + 2)
    width = up_to(4 * C * R, LANES)
    pack_rows = up_to(3 * R, 8)
    f32 = jnp.float32
    vmem = pltpu.VMEM
    edge_rows = 4 * (R + 2)
    dma = pltpu.SemaphoreType.DMA
    flat = lambda a: a.reshape(a.shape[0], -1)
    return pl.pallas_call(
        functools.partial(kernel, (M, G, K, R, C, V, O, J, QP)),
        out_shape=jax.ShapeDtypeStruct(ensemble.shape, f32),
        in_specs=[pl.BlockSpec(memory_space=pl.ANY)] + [pl.BlockSpec(memory_space=vmem)] * 3
        + [pl.BlockSpec(memory_space=pltpu.SMEM)],
        out_specs=pl.BlockSpec(memory_space=vmem),
        scratch_shapes=[
            vmem((members, R, C, V), f32),
            vmem((G * pack_rows, O), f32),
            vmem((C * pack_rows, O), f32),
            vmem((R, C, V), f32),
            vmem((R * J * C, O), f32),
            vmem((2 * R, C, O), f32),
            vmem((2 * targets, slots_all), jnp.bfloat16),
            vmem((QP, slots_all), jnp.bfloat16),
            vmem((QP, slots_all), jnp.bfloat16),
            vmem((targets, QP), f32),
            vmem((2, edge_rows, QP), f32),
            vmem((2, 4 * C, QP), f32),
            vmem((6, edge_rows, QP), f32),
            vmem((width, QP), f32),
            vmem((members, J, width), f32),
            vmem((members, J, width), f32),
            vmem((members, J, width), f32),
            vmem((2, J, width), f32),
            vmem((QP, width), f32),
            vmem((members, R, C, V), f32),
            dma((M,)), dma((M,)), dma((G,)), dma((G,)), dma((8,)), dma((8,)), dma((M,)), dma((M,)), dma((3,)),
        ],
        compiler_params=pltpu.CompilerParams(
            collective_id=0, has_side_effects=True, vmem_limit_bytes=56 * 1024 * 1024
        ),
    )(ensemble, flat(obs_value), flat(obs_error), flat(obs_index), obs_count.reshape(1, -1))


def solution(mesh):
    return jax.shard_map(
        functools.partial(local, mesh.shape["member"], mesh.shape["region"]),
        mesh=mesh,
        in_specs=(
            P("member", "region", None, None),
            P(None, ("member", "region"), None),
            P(None, ("member", "region"), None),
            P(None, ("member", "region"), None),
            P(None, ("member", "region")),
        ),
        out_specs=P("member", "region", None, None),
        check_vma=False,
    )
```

time: 173 us -> 28.2 us (0.16); the launches traced: 170 us -> 28 us
  matrix products: 79.8 us -> 0 us
  local copies, waits for them, and re-layouts: 35.4 us -> 1.78 us
  Pallas kernels: 0 us -> 26.2 us
  blocking collectives: 19.8 us -> 0 us
  waiting for transfers between devices: 16.1 us -> 0 us
  starting transfers between devices: 11.8 us -> 0 us
  other arithmetic: 3.63 us -> 0 us
  loops' own time: 3.01 us -> 0 us
    dot_general x178 -> x0, matrix products: 79.8 us -> none  [the longest x136 26.5 us: batch_product(): jnp.einsum('...ij,...jk->...ik', left, right, precision=lax.Precision.HIG...]
    pallas_call x0 -> x1, Pallas kernels: none -> 26.2 us  [local(): pl.pallas_call(functools.partial(kernel, (M, G, K, R, C, V, O, J, QP)), o...]
    all_to_all x1 -> x0, blocking collectives: 19.8 us -> none  [local(): lax.all_to_all(outgoing, ('member', 'region'), split_axis=0, concat_axis=...]
    all_to_all x1 -> x0, waiting for transfers between devices: 11.7 us -> none  [local(): lax.all_to_all(ensemble[None], ('member', 'region'), split_axis=3, concat...]
    transpose x8 -> x0, local copies, waits for them, and re-layouts: 11.2 us -> none  [analyze(): jnp.einsum('jrcvaybx,rcabjk->krcvaybx', shaped, point_weights, precision=...]
    another operation x16 -> x0, local copies, waits for them, and re-layouts: 9.86 us -> none
    reshape x13 -> x0, local copies, waits for them, and re-layouts: 9.83 us -> none  [the longest x8 9.01 us: analyze(): return ens_mean[None] + updated.reshape(anomaly.shape)]
    all_to_all x1 -> x0, starting transfers between devices: 6.35 us -> none  [local(): lax.all_to_all(ensemble[None], ('member', 'region'), split_axis=3, concat...]
  transfers between devices with their start and end apart: 3 -> 0, of which waited for: 3 -> 0; matrix products, arithmetic and copies ran while one was open for 0% -> 0% of each run, Pallas kernels for 0% -> 0%
where the time goes in v1:
time: 28.2 us; the launch traced here: 28 us
  Pallas kernels  26.2 us (93%)
  local copies, waits for them, and re-layouts  1.78 us (6%)
    pallas_call x1, Pallas kernels, local(): pl.pallas_call(functools.partial(kernel, (M, G, K, R, C, V, O, J, QP)), o...  26.2 us
    unnamed x1, local copies, waits for them, and re-layouts  1.78 us

profile of v1, /device:TPU:7, one launch (start us, length us, event | category | flops | bytes accessed | tf_op | source)
XLA Modules:
  0.0 28.0 jit_solution(192174490046510017)
XLA Ops:
  0.0 26.2 %shard_map.55 = f32[3,2,32,512]{3,2,1,0:T(8,128)} custom-call(f32[3,2,32,512]{3,2,1,0:T(8,128)} %ens_ref.1, f32[16,128]{1,0:T(8,128)} %bitcast.4, f32[16,128]{1,0:T(8,128)} %bitcast.5, s32[16,128]{1,0:T(8,128)} %bitcast.6, s32[1,16]{1,0:T(1,128)} %bitcast.7), custom_call_target="tpu_custom_call" | custom-call | tf_op jit(solution)/shard_map/pallas_call | solution.py:418
  26.2 1.8 %copy.7 = f32[3,2,32,512]{3,2,1,0:T(8,128)} copy(f32[3,2,32,512]{3,2,1,0:T(8,128)} %shard_map.55) | data formatting | bytes 786432

commit v2 on v1

--- a/solution.py
+++ b/solution.py
@@ -31,8 +31,8 @@
 
 def kernel(
     dims,
-    ens_ref, value_ref, error_ref, index_ref, count_ref, out_ref,
-    ens, pack, obs, mean, slots, place, loc, qhi, qlo, acc, side,
+    ens_ref, value_any, error_any, index_any, count_ref, out_ref,
+    value_ref, error_ref, index_ref, ens, pack, obs, mean, slots, place, loc, qhi, qlo, acc, side,
     row_in, side_in, prec, root, inv, step, small, weights, outgoing,
     ens_send, ens_recv, obs_send, obs_recv, halo_send, halo_recv, out_send, out_recv, local_sem,
 ):
@@ -45,6 +45,11 @@
     targets = 4 * C * (R + 2)
     f32 = jnp.float32
 
+    loads = []
+    for n, (src, dst) in enumerate(((value_any, value_ref), (error_any, error_ref), (index_any, index_ref))):
+        load = pltpu.make_async_copy(src, dst, local_sem.at[3 + n])
+        load.start()
+        loads.append(load)
     barrier = pltpu.get_barrier_semaphore()
     for off in range(1, M):
         pl.semaphore_signal(barrier, inc=1, device_id=(lax.rem(m + off, M), g), device_id_type=MESH)
@@ -70,6 +75,8 @@
         ens_ref.at[:, :, pl.ds(pl.multiple_of(m * C, C), C), :], ens.at[pl.ds(m * K, K)], local_sem.at[0]
     )
     own_ens.start()
+    for load in loads:
+        load.wait()
     slot = lax.broadcasted_iota(jnp.int32, (G * R, O), 1)
     slot_row = lax.broadcasted_iota(jnp.int32, (G * R, O), 0)
     count = jnp.zeros((G * R, O), jnp.int32)
@@ -338,7 +345,7 @@
     fields = V // CELLS
     band = HALF * SIDE
     left_half = (lax.broadcasted_iota(jnp.int32, (C, band), 1) & (SIDE - 1)) < HALF
-    for dest in range(M):
+    def update(dest):
         for i in range(R):
             for h in range(2):
                 first = (i * 4 + 2 * h) * C
@@ -376,6 +383,18 @@
         def _():
             pltpu.make_async_copy(outgoing.at[dest * K : (dest + 1) * K], target, local_sem.at[2]).start()
 
+    far = M // 2
+
+    @pl.when(m < far)
+    def _():
+        for dest in list(range(far, M)) + list(range(far)):
+            update(dest)
+
+    @pl.when(m >= far)
+    def _():
+        for dest in range(M):
+            update(dest)
+
     for copy in sends:
         copy.wait_send()
     for dm, dg, src, dst, n in plans:
@@ -417,11 +436,14 @@
     flat = lambda a: a.reshape(a.shape[0], -1)
     return pl.pallas_call(
         functools.partial(kernel, (M, G, K, R, C, V, O, J, QP)),
-        out_shape=jax.ShapeDtypeStruct(ensemble.shape, f32),
-        in_specs=[pl.BlockSpec(memory_space=pl.ANY)] + [pl.BlockSpec(memory_space=vmem)] * 3
+        out_shape=pltpu.VMEM(ensemble.shape, f32),
+        in_specs=[pl.BlockSpec(memory_space=pl.ANY)] * 4
         + [pl.BlockSpec(memory_space=pltpu.SMEM)],
         out_specs=pl.BlockSpec(memory_space=vmem),
         scratch_shapes=[
+            vmem((G * R, O), f32),
+            vmem((G * R, O), f32),
+            vmem((G * R, O), jnp.int32),
             vmem((members, R, C, V), f32),
             vmem((G * pack_rows, O), f32),
             vmem((C * pack_rows, O), f32),
@@ -442,7 +464,7 @@
             vmem((2, J, width), f32),
             vmem((QP, width), f32),
             vmem((members, R, C, V), f32),
-            dma((M,)), dma((M,)), dma((G,)), dma((G,)), dma((8,)), dma((8,)), dma((M,)), dma((M,)), dma((3,)),
+            dma((M,)), dma((M,)), dma((G,)), dma((G,)), dma((8,)), dma((8,)), dma((M,)), dma((M,)), dma((6,)),
         ],
         compiler_params=pltpu.CompilerParams(
             collective_id=0, has_side_effects=True, vmem_limit_bytes=56 * 1024 * 1024

time: 28.2 us -> 25.4 us (0.901)
  Pallas kernels: 26.2 us -> 24.3 us
  local copies, waits for them, and re-layouts: 1.78 us -> 0.75 us
    pallas_call x1, Pallas kernels: 26.2 us -> 24.3 us  [local(): pl.pallas_call(functools.partial(kernel, (M, G, K, R, C, V, O, J, QP)), o...]
    unnamed x1, local copies, waits for them, and re-layouts: 1.78 us -> 0.75 us
where the time goes in v2:
time: 25.4 us; the launch traced here: 25 us
  Pallas kernels  24.3 us (96%)
  local copies, waits for them, and re-layouts  0.75 us (3%)
    pallas_call x1, Pallas kernels, local(): pl.pallas_call(functools.partial(kernel, (M, G, K, R, C, V, O, J, QP)), o...  24.3 us
    unnamed x1, local copies, waits for them, and re-layouts  0.75 us

profile of v2, /device:TPU:7, one launch (start us, length us, event | category | flops | bytes accessed | tf_op | source)
XLA Modules:
  0.0 25.0 jit_solution(7485508575745694883)
XLA Ops:
  0.0 24.3 %shard_map.55 = f32[3,2,32,512]{3,2,1,0:T(8,128)S(1)} custom-call(f32[3,2,32,512]{3,2,1,0:T(8,128)} %ens_ref.1, f32[16,128]{1,0:T(8,128)} %bitcast.4, f32[16,128]{1,0:T(8,128)} %bitcast.5, s32[16,128]{1,0:T(8,128)} %bitcast.6, s32[1,16]{1,0:T(1,128)} %bitcast.7), custom_call_target="tpu_custom_call" | custom-call | tf_op jit(solution)/shard_map/pallas_call | solution.py:437
  24.3 0.7 %copy.7 = f32[3,2,32,512]{3,2,1,0:T(8,128)} copy(f32[3,2,32,512]{3,2,1,0:T(8,128)S(1)} %shard_map.55) | data formatting | bytes 786432

commit v3 on v2

--- a/solution.py
+++ b/solution.py
@@ -32,9 +32,10 @@
 def kernel(
     dims,
     ens_ref, value_any, error_any, index_any, count_ref, out_ref,
-    value_ref, error_ref, index_ref, ens, pack, obs, mean, slots, place, loc, qhi, qlo, acc, side,
-    row_in, side_in, prec, root, inv, step, small, weights, outgoing,
-    ens_send, ens_recv, obs_send, obs_recv, halo_send, halo_recv, out_send, out_recv, local_sem,
+    value_ref, error_ref, index_ref, ens, pack, obs, slots, place, loc, qhi, qlo, acc, side,
+    row_in, side_in, prec, root, inv, step, small, weights, came_weights,
+    ens_send, ens_recv, obs_send, obs_recv, halo_send, halo_recv, out_send, out_recv,
+    far_send, far_recv, pair_send, pair_recv, local_sem,
 ):
     M, G, K, R, C, V, O, J, QP = dims
     members = M * K
@@ -72,7 +73,7 @@
                     pl.semaphore_signal(barrier, inc=1, device_id=(m + dm, g + dg), device_id_type=MESH)
 
     own_ens = pltpu.make_async_copy(
-        ens_ref.at[:, :, pl.ds(pl.multiple_of(m * C, C), C), :], ens.at[pl.ds(m * K, K)], local_sem.at[0]
+        ens_ref, ens.at[pl.ds(m * K, K)], local_sem.at[0]
     )
     own_ens.start()
     for load in loads:
@@ -93,6 +94,9 @@
         pack[base + 2 * R : base + 3 * R, :] = index_f[d * R : (d + 1) * R]
         if pack_rows > 3 * R:
             pack[base + 3 * R : base + pack_rows, :] = jnp.zeros((pack_rows - 3 * R, O), f32)
+    if weights.shape[1] > members * K:
+        tail = weights.shape[1] - members * K
+        weights[:, members * K :, :] = jnp.zeros((M, tail, weights.shape[2]), f32)
     if QP > members * J:
         qhi[members * J :, :] = jnp.zeros((QP - members * J, qhi.shape[1]), jnp.bfloat16)
         qlo[members * J :, :] = jnp.zeros((QP - members * J, qlo.shape[1]), jnp.bfloat16)
@@ -100,13 +104,73 @@
     sides = jnp.where(m > 0, 1, 0) + jnp.where(m < M - 1, 1, 0)
     ends = jnp.where(g > 0, 1, 0) + jnp.where(g < G - 1, 1, 0)
     pl.semaphore_wait(barrier, M - 1 + G - 1 + sides * ends)
+
+    def block(ref, owner, group):
+        columns = pl.ds(pl.multiple_of(group * C, C), C)
+        if owner is None:
+            return ref.at[:, :, columns, :]
+        return ref.at[pl.ds(owner * K, K), :, columns, :]
+
+    def move(src, dst, to, send, recv, n):
+        return pltpu.make_async_remote_copy(
+            src_ref=src, dst_ref=dst, send_sem=send.at[n], recv_sem=recv.at[n],
+            device_id=(to, g), device_id_type=MESH,
+        )
+
+    chips = M // 2
+    chip = m // 2
+    core = lax.rem(m, 2)
+    pal = chip * 2 + 1 - core
+    rest_out, rest_in, own_out, own_in, near_out, near_in, last_out, last_in = [[] for _ in range(8)]
+    slot_no = 0
+    for off in range(1, M):
+        group = lax.rem(pal + off, M)
+        mine = lax.rem(m + off, M)
+        own_out.append(move(block(ens_ref, None, group), block(ens, m, group), pal, pair_send, pair_recv, slot_no))
+        own_in.append(move(block(ens_ref, None, mine), block(ens, pal, mine), pal, pair_send, pair_recv, slot_no))
+        slot_no += 1
+    for co in range(1, chips):
+        away = lax.rem(chip + co, chips)
+        back = lax.rem(chip + chips - co, chips)
+        for flip in range(2):
+            lane_core = core if flip == 0 else 1 - core
+            pal_core = 1 - core if flip == 0 else core
+            near_out.append(move(
+                block(ens, away * 2 + lane_core, m), block(ens, away * 2 + lane_core, m),
+                pal, pair_send, pair_recv, slot_no,
+            ))
+            near_in.append(move(
+                block(ens, away * 2 + pal_core, pal), block(ens, away * 2 + pal_core, pal),
+                pal, pair_send, pair_recv, slot_no,
+            ))
+            slot_no += 1
+        for po in range(1, chips):
+            for cc in range(2):
+                n = ((co - 1) * (chips - 1) + po - 1) * 2 + cc
+                group = lax.rem(away + po, chips) * 2 + cc
+                mine = lax.rem(chip + po, chips) * 2 + cc
+                rest_out.append(move(
+                    block(ens_ref, None, group), block(ens, m, group), away * 2 + core, far_send, far_recv, n
+                ))
+                rest_in.append(move(
+                    block(ens_ref, None, mine), block(ens, back * 2 + core, mine), back * 2 + core, far_send, far_recv, n
+                ))
+                last_out.append(move(
+                    block(ens, back * 2 + core, mine), block(ens, back * 2 + core, mine),
+                    pal, pair_send, pair_recv, slot_no,
+                ))
+                last_in.append(move(
+                    block(ens, back * 2 + 1 - core, mine), block(ens, back * 2 + 1 - core, mine),
+                    pal, pair_send, pair_recv, slot_no,
+                ))
+                slot_no += 1
 
     sends = []
     for off in range(1, M):
         to = lax.rem(m + off, M)
         copy = pltpu.make_async_remote_copy(
             src_ref=ens_ref.at[:, :, pl.ds(pl.multiple_of(to * C, C), C), :],
-            dst_ref=ens.at[pl.ds(m * K, K)],
+            dst_ref=block(ens, m, to),
             send_sem=ens_send.at[off], recv_sem=ens_recv.at[off],
             device_id=(to, g), device_id_type=MESH,
         )
@@ -125,13 +189,16 @@
         )
         copy.start()
         sends.append(copy)
+    early = len(rest_out) // 2
+    for copy in own_out + rest_out[:early]:
+        copy.start()
     own_ens.wait()
     own_obs.wait()
     for off in range(1, M):
         came = lax.rem(m + M - off, M)
         pltpu.make_async_remote_copy(
             src_ref=ens_ref.at[:, :, pl.ds(pl.multiple_of(m * C, C), C), :],
-            dst_ref=ens.at[pl.ds(came * K, K)],
+            dst_ref=block(ens, came, m),
             send_sem=ens_send.at[off], recv_sem=ens_recv.at[off],
             device_id=(came, g), device_id_type=MESH,
         ).wait_recv()
@@ -144,6 +211,9 @@
             device_id=(m, came), device_id_type=MESH,
         ).wait_recv()
 
+    for copy in near_out:
+        copy.start()
+
     tiles = V // LANES
     for i in range(R):
         wgt = obs[pl.ds(i, C, stride=pack_rows), :]
@@ -162,15 +232,15 @@
                 got = jnp.where(tile == t, more, got)
             return got
 
-        total = ens[0, i]
+        here_cols = pl.ds(pl.multiple_of(m * C, C), C)
+        total = ens[0, i, here_cols, :]
         for k in range(1, members):
-            total = total + ens[k, i]
+            total = total + ens[k, i, here_cols, :]
         avg = total * (1.0 / members)
-        mean[i] = avg
         seen_mean = seen(avg)
         base = i * J * C
         for k in range(members):
-            slots[base + k * C : base + (k + 1) * C, :] = wgt * (seen(ens[k, i]) - seen_mean)
+            slots[base + k * C : base + (k + 1) * C, :] = wgt * (seen(ens[k, i, here_cols, :]) - seen_mean)
         slots[base + members * C : base + (members + 1) * C, :] = wgt * (val - seen_mean)
         if J > members + 1:
             slots[base + (members + 1) * C : base + J * C, :] = jnp.zeros(((J - members - 1) * C, O), f32)
@@ -240,6 +310,8 @@
                 src_ref=src, dst_ref=dst, send_sem=halo_send.at[n], recv_sem=halo_recv.at[n],
                 device_id=(m + dm, g + dg), device_id_type=MESH,
             ).start()
+    for copy in rest_out[early:]:
+        copy.start()
     for dm, dg, src, dst, n in plans:
         @pl.when(near[-dm, -dg])
         def _():
@@ -337,27 +409,45 @@
         mean_w = mean_w + small[0, i : i + 1, :] * inv_root[i]
     small[1] = mean_w
     for j in range(members):
-        weights[j * J : (j + 1) * J, :] = small[1, j : j + 1, :] + math.sqrt(members - 1) * inv_root[j]
-    if QP > members * J:
-        weights[members * J :, :] = jnp.zeros((QP - members * J, width), f32)
-    prec[...] = jnp.transpose(weights[...])
+        all_k = small[1, j : j + 1, :] + math.sqrt(members - 1) * inv_root[j]
+        for dest in range(M):
+            weights[dest, j * K : (j + 1) * K, :] = all_k[dest * K : (dest + 1) * K]
+
+    weight_moves = []
+    for off in range(1, M):
+        to = lax.rem(m + off, M)
+        copy = move(weights.at[to], came_weights.at[m], to, out_send, out_recv, off)
+        copy.start()
+        weight_moves.append(copy)
+    for copy in rest_in:
+        copy.wait_recv()
+    for copy in last_out:
+        copy.start()
 
     fields = V // CELLS
     band = HALF * SIDE
     left_half = (lax.broadcasted_iota(jnp.int32, (C, band), 1) & (SIDE - 1)) < HALF
-    def update(dest):
+
+    def update(group, turned):
+        columns = pl.ds(pl.multiple_of(group * C, C), C)
         for i in range(R):
             for h in range(2):
                 first = (i * 4 + 2 * h) * C
-                west = prec[first : first + C, :]
-                east = prec[first + C : first + 2 * C, :]
+                west = turned[first : first + C]
+                east = turned[first + C : first + 2 * C]
                 lanes = [f * CELLS + h * band for f in range(fields)]
-                avgs = [mean[i, :, a : a + band] for a in lanes]
+                raw = [[ens[j, i, columns, a : a + band] for a in lanes] for j in range(members)]
+                avgs = []
+                for f in range(fields):
+                    total = raw[0][f]
+                    for j in range(1, members):
+                        total = total + raw[j][f]
+                    avgs.append(total * (1.0 / members))
                 outs = [[avgs[f] for f in range(fields)] for _ in range(K)]
                 for j in range(members):
-                    anoms = [ens[j, i, :, a : a + band] - avgs[f] for f, a in enumerate(lanes)]
+                    anoms = [raw[j][f] - avgs[f] for f in range(fields)]
                     for kk in range(K):
-                        q = j * J + dest * K + kk
+                        q = j * K + kk
                         w = jnp.where(
                             left_half,
                             jnp.broadcast_to(west[:, q : q + 1], (C, band)),
@@ -367,34 +457,17 @@
                             outs[kk][f] = outs[kk][f] + anoms[f] * w
                 for kk in range(K):
                     for f, a in enumerate(lanes):
-                        outgoing[dest * K + kk, i, :, a : a + band] = outs[kk][f]
-        away = lax.rem(dest - m + M, M)
-        target = out_ref.at[:, :, pl.ds(pl.multiple_of(m * C, C), C), :]
-
-        @pl.when(away != 0)
-        def _():
-            pltpu.make_async_remote_copy(
-                src_ref=outgoing.at[dest * K : (dest + 1) * K], dst_ref=target,
-                send_sem=out_send.at[away], recv_sem=out_recv.at[away],
-                device_id=(dest, g), device_id_type=MESH,
-            ).start()
-
-        @pl.when(away == 0)
-        def _():
-            pltpu.make_async_copy(outgoing.at[dest * K : (dest + 1) * K], target, local_sem.at[2]).start()
-
-    far = M // 2
-
-    @pl.when(m < far)
-    def _():
-        for dest in list(range(far, M)) + list(range(far)):
-            update(dest)
-
-    @pl.when(m >= far)
-    def _():
-        for dest in range(M):
-            update(dest)
-
+                        out_ref[kk, i, columns, a : a + band] = outs[kk][f]
+
+    update(m, jnp.transpose(weights[m]))
+    for copy in own_in + near_in + last_in:
+        copy.wait_recv()
+    for off in range(1, M):
+        came = lax.rem(m + M - off, M)
+        move(weights.at[m], came_weights.at[came], came, out_send, out_recv, off).wait_recv()
+        update(came, jnp.transpose(came_weights[came]))
+
+    sends += own_out + rest_out + near_out + last_out + weight_moves
     for copy in sends:
         copy.wait_send()
     for dm, dg, src, dst, n in plans:
@@ -404,18 +477,6 @@
                 src_ref=src, dst_ref=dst, send_sem=halo_send.at[n], recv_sem=halo_recv.at[n],
                 device_id=(m + dm, g + dg), device_id_type=MESH,
             ).wait_send()
-    pltpu.make_async_copy(
-        outgoing.at[pl.ds(m * K, K)], out_ref.at[:, :, pl.ds(pl.multiple_of(m * C, C), C), :], local_sem.at[2]
-    ).wait()
-    for off in range(1, M):
-        to = lax.rem(m + off, M)
-        came = lax.rem(m + M - off, M)
-        pltpu.make_async_remote_copy(
-            src_ref=outgoing.at[pl.ds(to * K, K)],
-            dst_ref=out_ref.at[:, :, pl.ds(pl.multiple_of(came * C, C), C), :],
-            send_sem=out_send.at[off], recv_sem=out_recv.at[off],
-            device_id=(to, g), device_id_type=MESH,
-        ).wait()
 
 
 def local(M, G, ensemble, obs_value, obs_error, obs_index, obs_count):
@@ -432,6 +493,10 @@
     f32 = jnp.float32
     vmem = pltpu.VMEM
     edge_rows = 4 * (R + 2)
+    WR = up_to(members * K, 8)
+    chips = M // 2
+    far = 2 * (chips - 1) ** 2
+    pair = M - 1 + 2 * (chips - 1) + far
     dma = pltpu.SemaphoreType.DMA
     flat = lambda a: a.reshape(a.shape[0], -1)
     return pl.pallas_call(
@@ -444,10 +509,9 @@
             vmem((G * R, O), f32),
             vmem((G * R, O), f32),
             vmem((G * R, O), jnp.int32),
-            vmem((members, R, C, V), f32),
+            vmem((members, R, cols, V), f32),
             vmem((G * pack_rows, O), f32),
             vmem((C * pack_rows, O), f32),
-            vmem((R, C, V), f32),
             vmem((R * J * C, O), f32),
             vmem((2 * R, C, O), f32),
             vmem((2 * targets, slots_all), jnp.bfloat16),
@@ -462,9 +526,10 @@
             vmem((members, J, width), f32),
             vmem((members, J, width), f32),
             vmem((2, J, width), f32),
-            vmem((QP, width), f32),
-            vmem((members, R, C, V), f32),
-            dma((M,)), dma((M,)), dma((G,)), dma((G,)), dma((8,)), dma((8,)), dma((M,)), dma((M,)), dma((6,)),
+            vmem((M, WR, width), f32),
+            vmem((M, WR, width), f32),
+            dma((M,)), dma((M,)), dma((G,)), dma((G,)), dma((8,)), dma((8,)), dma((M,)), dma((M,)),
+            dma((far,)), dma((far,)), dma((pair,)), dma((pair,)), dma((6,)),
         ],
         compiler_params=pltpu.CompilerParams(
             collective_id=0, has_side_effects=True, vmem_limit_bytes=56 * 1024 * 1024

time: 25.4 us -> 24.5 us (0.965)
  the two profiles are of different devices: /device:TPU:7 before, /device:TPU:0 now
where the time goes in v3:
time: 24.5 us; the launch traced here: 24.3 us
  Pallas kernels  23.6 us (96%)
  local copies, waits for them, and re-layouts  0.75 us (3%)
    pallas_call x1, Pallas kernels, local(): pl.pallas_call(functools.partial(kernel, (M, G, K, R, C, V, O, J, QP)), o...  23.6 us
    unnamed x1, local copies, waits for them, and re-layouts  0.75 us

profile of v3, /device:TPU:0, one launch (start us, length us, event | category | flops | bytes accessed | tf_op | source)
XLA Modules:
  0.0 24.3 jit_solution(10199837312391641457)
XLA Ops:
  0.0 23.6 %shard_map.55 = f32[3,2,32,512]{3,2,1,0:T(8,128)S(1)} custom-call(f32[3,2,32,512]{3,2,1,0:T(8,128)} %ens_ref.1, f32[16,128]{1,0:T(8,128)} %bitcast.4, f32[16,128]{1,0:T(8,128)} %bitcast.5, s32[16,128]{1,0:T(8,128)} %bitcast.6, s32[1,16]{1,0:T(1,128)} %bitcast.7), custom_call_target="tpu_custom_call" | custom-call | tf_op jit(solution)/shard_map/pallas_call | solution.py:502
  23.6 0.7 %copy.7 = f32[3,2,32,512]{3,2,1,0:T(8,128)} copy(f32[3,2,32,512]{3,2,1,0:T(8,128)S(1)} %shard_map.55) | data formatting | bytes 786432
